TPU v7x, 32 devices: a whole 2x2x4 slice. The times are simulated.
32 devices in a mesh: groups: 2 (over x), ctx: 16 (over z, y, core).
Axes of the slice: x: 2, y: 2, z: 4, core: 2. Of those that a mesh axis runs over, the one named last changes fastest.
Arguments:
- queries: bfloat16 [96, 4096], P(('groups', 'ctx')), parts along dimension 0, may hold values from -200 to 200
- cache_keys: bfloat16 [4096, 512], P(('groups', 'ctx')), parts along dimension 0, may hold values from -6 to 6
- cache_values: bfloat16 [4096, 512], P(('groups', 'ctx')), parts along dimension 0, may hold values from -6 to 6
- new_keys: bfloat16 [96, 512], P(('groups', 'ctx')), parts along dimension 0, may hold values from -6 to 6
- new_values: bfloat16 [96, 512], P(('groups', 'ctx')), parts along dimension 0, may hold values from -6 to 6
- cache_lengths: int32 [32], P(('groups', 'ctx')), parts along dimension 0, may hold values from 0 to 128, as said below
- residual_in: bfloat16 [96, 2048], P(('groups', 'ctx')), parts along dimension 0, may hold values from -6 to 6
- out_weight: bfloat16 [4096, 2048], P('ctx'), may hold values from -3 to 3
- norm_gain: bfloat16 [2048], replicated, may hold values from 0.25 to 1.75
- expert_gate: bfloat16 [16, 2048, 768], P('ctx'), may hold values from -0.125 to 0.125
- expert_up: bfloat16 [16, 2048, 768], P('ctx'), may hold values from -0.125 to 0.125
- expert_down: bfloat16 [16, 768, 2048], P('ctx'), may hold values from -0.21875 to 0.21875
- expert_ids: int32 [96, 8], P(('groups', 'ctx')), parts along dimension 0, may hold values from 0 to 15, all different within a row; in each aligned block of 3 rows (0 to 2, 3 to 5, ...) at most 3 rows name the same one
- expert_weights: float32 [96, 8], P(('groups', 'ctx')), parts along dimension 0, may hold values from 0.03 to 0.4
Outputs:
- layer_out: bfloat16 [96, 2048], P(('groups', 'ctx')), parts along dimension 0
There are 2 independent parts, one for each index of `groups`. A program takes and returns all parts, laid end to end along the dimension named above; an argument that names none is the same for every part. Nothing has to cross between parts.
Inputs may be any that keep to these rules, and one draw needn't show every extreme that they name: `cache_lengths`: some shard in every draw is full, with 128 live positions. `expert_ids`: within one block of 3 rows no expert is named more than 3 times, a bound that some block reaches.
All inputs are finite; a program needn't handle non-finite values.
Results may differ from a plain program's by a relative error of at most 0.01.
Values may be sent and summed in bfloat16 or wider, within the bound.
No kernel may reach another device: no remote copies, remote signals or barrier semaphores. Data moves between devices by JAX's collectives and lax.ppermute only.
A program may use at most 64 MiB of HBM per device.

v0:
```python
import jax
import jax.numpy as jnp
from jax import lax
from jax.sharding import PartitionSpec as P

HEADS = 32
KV_HEADS = 4
HEAD_DIM = 128
TOP = 8


MASKED = -1e30
epsilon = 1e-06


def local(
    queries,
    cache_keys,
    cache_values,
    new_keys,
    new_values,
    cache_lengths,
    residual_in,
    out_weight,
    norm_gain,
    expert_gate,
    expert_up,
    expert_down,
    expert_ids,
    expert_weights,
):
    shards = lax.axis_size("ctx")
    device = lax.axis_index("ctx")
    rows_dev = residual_in.shape[0]
    capacity = max(2, 2 * rows_dev * TOP // shards)
    group_size = HEADS // KV_HEADS
    whole_queries = lax.all_gather(queries, "ctx", axis=0, tiled=True)
    all_rows = whole_queries.shape[0]
    query_heads = whole_queries.reshape(all_rows, KV_HEADS, group_size, HEAD_DIM)
    local_cache = cache_keys.shape[0]
    key_rows = jnp.concatenate([cache_keys, new_keys], 0).reshape(
        local_cache + rows_dev, KV_HEADS, HEAD_DIM
    )
    value_rows = jnp.concatenate([cache_values, new_values], 0).reshape(
        local_cache + rows_dev, KV_HEADS, HEAD_DIM
    )
    slot_ids = jnp.arange(local_cache + rows_dev, dtype=jnp.int32)
    span_pos = device * rows_dev + slot_ids - local_cache
    row_ids = jnp.arange(all_rows, dtype=jnp.int32)
    usable = jnp.where(
        slot_ids[None, :] < local_cache,
        (slot_ids < cache_lengths[0])[None, :],
        span_pos[None, :] <= row_ids[:, None],
    )
    scores = jnp.einsum(
        "rkgd,nkd->kgrn", query_heads, key_rows, preferred_element_type=jnp.float32
    ) * HEAD_DIM ** (-0.5)
    scores = jnp.where(usable, scores, MASKED)
    maxima = jnp.max(scores, axis=-1)
    exp_weights = jnp.where(usable, jnp.exp(scores - maxima[..., None]), 0.0)
    totals = jnp.sum(exp_weights, axis=-1)
    numerators = jnp.einsum(
        "kgrn,nkd->rkgd",
        exp_weights.astype(jnp.bfloat16),
        value_rows,
        preferred_element_type=jnp.float32,
    ).reshape(all_rows, HEADS, HEAD_DIM)
    maxima = maxima.transpose(2, 0, 1).reshape(all_rows, HEADS)
    totals = totals.transpose(2, 0, 1).reshape(all_rows, HEADS)
    largest = lax.pmax(maxima, "ctx")
    rescale = jnp.exp(maxima - largest)
    denoms = lax.psum(totals * rescale, "ctx")
    weighted = (numerators * (rescale / denoms)[..., None]).reshape(all_rows, HEADS * HEAD_DIM)
    columns = lax.psum_scatter(weighted, "ctx", scatter_dimension=1, tiled=True).astype(
        jnp.bfloat16
    )
    projected = lax.psum_scatter(
        jnp.dot(columns, out_weight, preferred_element_type=jnp.float32),
        "ctx",
        scatter_dimension=0,
        tiled=True,
    )
    state = residual_in.astype(jnp.float32) + projected
    normed = (
        state
        * lax.rsqrt(jnp.mean(state * state, axis=1, keepdims=True) + epsilon)
        * norm_gain.astype(jnp.float32)
    ).astype(jnp.bfloat16)
    n_slots = shards * capacity
    flat_ids = expert_ids.reshape(-1)
    places = jnp.arange(flat_ids.shape[0], dtype=jnp.int32)
    earlier = (flat_ids[:, None] == flat_ids[None, :]) & (places[None, :] < places[:, None])
    slot_of = flat_ids * capacity + jnp.sum(earlier.astype(jnp.int32), axis=1)
    one_hot = (slot_of[:, None] == jnp.arange(n_slots, dtype=jnp.int32)[None, :]).astype(
        jnp.float32
    )
    dispatch_map = one_hot.reshape(rows_dev, TOP, n_slots).sum(1)
    outgoing = (
        jnp.dot(dispatch_map.T.astype(jnp.bfloat16), normed, preferred_element_type=jnp.float32)
        .astype(jnp.bfloat16)
        .reshape(shards, capacity, normed.shape[1])
    )
    received = lax.all_to_all(outgoing, "ctx", split_axis=0, concat_axis=0, tiled=True)
    gate_out = jnp.einsum(
        "scd,df->scf", received, expert_gate[0], preferred_element_type=jnp.float32
    )
    up_out = jnp.einsum("scd,df->scf", received, expert_up[0], preferred_element_type=jnp.float32)
    activated = (jax.nn.silu(gate_out) * up_out).astype(jnp.bfloat16)
    expert_out = jnp.einsum(
        "scf,fd->scd", activated, expert_down[0], preferred_element_type=jnp.float32
    ).astype(jnp.bfloat16)
    back = lax.all_to_all(expert_out, "ctx", split_axis=0, concat_axis=0, tiled=True)
    combine_map = (
        (one_hot * expert_weights.reshape(-1)[:, None]).reshape(rows_dev, TOP, n_slots).sum(1)
    )
    expert_sum = jnp.dot(
        combine_map,
        back.reshape(n_slots, normed.shape[1]).astype(jnp.float32),
        precision=lax.Precision.HIGHEST,
    )
    return (state + expert_sum).astype(jnp.bfloat16)


def solution(mesh):
    placed = (
        P(("groups", "ctx"), None),
        P(("groups", "ctx"), None),
        P(("groups", "ctx"), None),
        P(("groups", "ctx"), None),
        P(("groups", "ctx"), None),
        P(("groups", "ctx")),
        P(("groups", "ctx"), None),
        P("ctx", None),
        P(),
        P("ctx", None, None),
        P("ctx", None, None),
        P("ctx", None, None),
        P(("groups", "ctx"), None),
        P(("groups", "ctx"), None),
    )
    return jax.shard_map(
        local, mesh=mesh, in_specs=placed, out_specs=P(("groups", "ctx"), None), check_vma=False
    )
```

profile of v0, /device:TPU:0, one launch (start us, length us, event | category | flops | bytes accessed | tf_op | source)
XLA Modules:
  0.0 359.6 jit_solution(11415697979822261193)
XLA Ops:
  7.3 0.6 add_add_fusion
  7.9 0.6 iota_compare_fusion.3
  8.5 0.9 pad_maximum_fusion.1
  9.5 0.9 pad_maximum_fusion
  10.5 0.1 reshape.87
  10.6 26.4 %all-gather = bf16[16,3,4096]{2,1,0:T(4,128)(2,1)} all-gather(bf16[1,3,4096]{2,1,0:T(4,128)(2,1)} %bitcast.55), channel_id=1, replica_groups=mesh['groups'=2,'ctx'=16] {'ctx'}, dimensions={0}, use_global_device_ids=true | all-gather | bytes 417792 | tf_op jit(solution)/shard_map/all_gather | solution.py:37
  37.0 2.2 reshape.89
  39.2 0.7 fusion.36
  39.9 2.6 fusion.46
  42.5 57.8 %pmax.7 = f32[48,32]{0,1:T(8,128)S(1)} all-reduce(f32[48,32]{0,1:T(8,128)S(1)} %bitcast.53), channel_id=1, replica_groups=mesh['groups'=2,'ctx'=16] {'ctx'}, use_global_device_ids=true, to_apply=%region_1.2 | all-reduce | flops 1536 | bytes 12288 | tf_op jit(solution)/shard_map/pmax | solution.py:70
  100.3 2.1 fusion.10
  102.3 0.4 convolution_bitcast_fusion
  102.8 1.1 copy.35
  103.9 57.6 %psum.7 = f32[48,32]{0,1:T(8,128)S(1)} all-reduce(f32[48,32]{0,1:T(8,128)S(1)} %bitcast_multiply_fusion.1), channel_id=1, replica_groups=mesh['groups'=2,'ctx'=16] {'ctx'}, use_global_device_ids=true, to_apply=%region_3.4 | all-reduce | flops 1536 | bytes 12288 | tf_op jit(solution)/shard_map/psum | solution.py:72
  161.7 0.3 mul.72
  161.9 3.1 bitcast_multiply_fusion
  165.2 0.2 convert_reduce_fusion.1
  165.5 53.7 %reduce-scatter.2.cloned.1.call-done = f32[48,256]{1,0:T(8,128)} async-done(((f32[48,4096]{1,0:T(8,128)}), f32[48,256]{1,0:T(8,128)}) %reduce-scatter.2.cloned.1.call-update) | async-done | bytes 49168 | tf_op jit(solution)/shard_map/reduce_scatter | solution.py:74
  219.2 2.3 fusion.37
  221.6 0.6 dynamic-slice
  222.8 0.7 convert_reduce_fusion
  223.5 89.5 %all-reduce.3.cloned.1.call-done = f32[48,2048]{1,0:T(8,128)} async-done(((f32[48,2048]{1,0:T(8,128)}), f32[48,2048]{1,0:T(8,128)}) %all-reduce.3.cloned.1.call-update) | async-done | bytes 393232
  313.0 1.0 multiply_reduce_fusion
  314.0 1.2 convolution_convert_fusion
  315.2 0.8 reshape.93
  316.0 13.8 %all_to_all.10 = bf16[16,3,2048]{2,1,0:T(4,128)(2,1)S(1)} all-to-all(bf16[16,3,2048]{2,1,0:T(4,128)(2,1)} %reshape.93), channel_id=1, replica_groups=mesh['groups'=2,'ctx'=16] {'ctx'}, dimensions={0} | all-to-all | bytes 393216 | tf_op jit(solution)/shard_map/all_to_all | solution.py:103
  329.8 2.6 fusion.4
  332.4 3.9 %fusion.6 = bf16[16,3,2048]{2,0,1:T(8,128)(2,1)} fusion(bf16[1,768,2048]{2,1,0:T(8,128)(2,1)S(1)} %copy-done, bf16[1,2048,768]{2,1,0:T(8,128)(2,1)} %param.24, f32[16,3,768]{2,0,1:T(8,128)S(1)} %fusion.4, bf16[16,3,2048]{2,1,0:T(4,128)(2,1)S(1)} %all_to_all.10), kind=kOutput, calls=%fused_computation.6 | convolution fusion | flops 302309376 | bytes 6832128 | tf_op jit(solution)/shard_map/scf,fd->scd/dot_general | solution.py:109
  336.3 1.1 copy.39
  337.4 12.7 %all_to_all.11 = bf16[16,3,2048]{2,1,0:T(4,128)(2,1)S(1)} all-to-all(bf16[16,3,2048]{2,1,0:T(4,128)(2,1)S(1)} %copy.39), channel_id=1, replica_groups=mesh['groups'=2,'ctx'=16] {'ctx'}, dimensions={0} | all-to-all | bytes 393216 | tf_op jit(solution)/shard_map/all_to_all | solution.py:112
  350.1 0.8 reshape.94
  351.0 1.8 fusion.9
  (27 shorter events, 0.5 us)
Async XLA Ops:
  6.5 325.9 %copy-start = (bf16[1,768,2048]{2,1,0:T(8,128)(2,1)S(1)}, bf16[1,768,2048]{2,1,0:T(8,128)(2,1)}, u32[]{:S(2)}) copy-start(bf16[1,768,2048]{2,1,0:T(8,128)(2,1)} %param.25) | copy-start | bytes 9437188
  6.5 212.7 %reduce-scatter.2.cloned.1.call-start = ((), (), s32[]{:S(2)}) async-start(), calls=%async_computation.3 | async-start | bytes 835584 | tf_op jit(solution)/shard_map/reduce_scatter | solution.py:74
  100.3 2.1 copy-start.1
  161.9 3.2 copy-start.3
  165.0 56.5 %copy-start.4 = (bf16[2048]{0:T(1024)(128)(2,1)S(1)}, bf16[2048]{0:T(1024)(128)(2,1)}, u32[]{:S(2)}) copy-start(bf16[2048]{0:T(1024)(128)(2,1)} %param.22) | copy-start | bytes 12292
  165.0 56.5 %copy-start.6 = (u32[32]{0:T(128)S(1)}, u32[32]{0:T(128)}, u32[]{:S(2)}) copy-start(u32[32]{0:T(128)} %constant.43) | copy-start | bytes 388
  165.0 57.8 %copy-start.5 = (f32[3,8]{1,0:T(4,128)S(1)}, f32[3,8]{1,0:T(4,128)}, u32[]{:S(2)}) copy-start(f32[3,8]{1,0:T(4,128)} %param.27) | copy-start | bytes 292
  165.0 147.9 %copy-start.2 = (bf16[3,2048]{1,0:T(4,128)(2,1)S(1)}, bf16[3,2048]{1,0:T(4,128)(2,1)}, u32[]{:S(2)}) copy-start(bf16[3,2048]{1,0:T(4,128)(2,1)} %param.20) | copy-start | bytes 36868
  165.1 147.9 %all-reduce.3.cloned.1.call-start = ((), (), s32[]{:S(2)}) async-start(), calls=%async_computation.4 | async-start | bytes 786432
Sparse Core Ops, SparseCore 0:
  165.2 53.9 reduce-scatter.1
  222.5 90.3 all-reduce.2
where the time goes:
time: 360 us
  blocking collectives  168 us (47%)
  waiting for transfers between devices  143 us (40%)
  between operations  15 us (4%)
  matrix products  14.8 us (4%)
  other arithmetic  10.8 us (3%)
  local copies, waits for them, and re-layouts  7.41 us (2%)
    unnamed x3, waiting for transfers between devices  89.5 us
    pmax x1, blocking collectives, local(): largest = lax.pmax(maxima, 'ctx')  57.8 us
    psum x1, blocking collectives, local(): denoms = lax.psum(totals * rescale, 'ctx')  57.6 us
    reduce_scatter x1, waiting for transfers between devices, local(): lax.psum_scatter(weighted, 'ctx', scatter_dimension=1, tiled=True)  53.7 us
    all_gather x1, blocking collectives, local(): whole_queries = lax.all_gather(queries, 'ctx', axis=0, tiled=True)  26.4 us
    all_to_all x1, blocking collectives, local(): lax.all_to_all(outgoing, 'ctx', split_axis=0, concat_axis=0, tiled=True)  13.8 us
    all_to_all x1, blocking collectives, local(): lax.all_to_all(expert_out, 'ctx', split_axis=0, concat_axis=0, tiled=True)  12.7 us
  transfers between devices with their start and end apart: 2, of which 2 were waited for; matrix products, arithmetic and copies ran while one was open for 0% of the time, Pallas kernels for 0%

commit v1 on v0

v1 whole, which is shorter than its diff:
```python
import jax
import jax.numpy as jnp
from jax import lax
from jax.sharding import PartitionSpec as P

HEADS = 32
KV_HEADS = 4
HEAD_DIM = 128
TOP = 8


MASKED = -1e30
epsilon = 1e-06


def spread(block, shards):
    copies = jnp.broadcast_to(block[None], (shards,) + block.shape)
    return lax.all_to_all(copies, "ctx", split_axis=0, concat_axis=0, tiled=True)


def local(
    queries,
    cache_keys,
    cache_values,
    new_keys,
    new_values,
    cache_lengths,
    residual_in,
    out_weight,
    norm_gain,
    expert_gate,
    expert_up,
    expert_down,
    expert_ids,
    expert_weights,
):
    shards = lax.axis_size("ctx")
    device = lax.axis_index("ctx")
    rows_dev, width = residual_in.shape
    all_rows = rows_dev * shards
    group_size = HEADS // KV_HEADS
    columns_dev = out_weight.shape[0]
    whole_queries = spread(queries, shards).reshape(all_rows, HEADS * HEAD_DIM)
    query_heads = whole_queries.reshape(all_rows, KV_HEADS, group_size, HEAD_DIM)
    local_cache = cache_keys.shape[0]
    key_rows = jnp.concatenate([cache_keys, new_keys], 0).reshape(
        local_cache + rows_dev, KV_HEADS, HEAD_DIM
    )
    value_rows = jnp.concatenate([cache_values, new_values], 0).reshape(
        local_cache + rows_dev, KV_HEADS, HEAD_DIM
    )
    slot_ids = jnp.arange(local_cache + rows_dev, dtype=jnp.int32)
    span_pos = device * rows_dev + slot_ids - local_cache
    row_ids = jnp.arange(all_rows, dtype=jnp.int32)
    usable = jnp.where(
        slot_ids[None, :] < local_cache,
        (slot_ids < cache_lengths[0])[None, :],
        span_pos[None, :] <= row_ids[:, None],
    )
    scores = jnp.einsum(
        "rkgd,nkd->kgrn", query_heads, key_rows, preferred_element_type=jnp.float32
    ) * HEAD_DIM ** (-0.5)
    scores = jnp.where(usable, scores, MASKED)
    maxima = jnp.max(scores, axis=-1).astype(jnp.bfloat16)
    exp_weights = jnp.where(
        usable, jnp.exp(scores - maxima.astype(jnp.float32)[..., None]), 0.0
    )
    totals = jnp.sum(exp_weights, axis=-1)
    numerators = jnp.einsum(
        "kgrn,nkd->rkgd",
        exp_weights.astype(jnp.bfloat16),
        value_rows,
        preferred_element_type=jnp.float32,
    ).reshape(all_rows, HEADS * HEAD_DIM)
    maxima = maxima.transpose(2, 0, 1).reshape(all_rows, HEADS)
    totals = totals.transpose(2, 0, 1).reshape(all_rows, HEADS)
    totals_high = totals.astype(jnp.bfloat16)
    totals_low = (totals - totals_high.astype(jnp.float32)).astype(jnp.bfloat16)
    heads_dev = max(1, columns_dev // HEAD_DIM)
    repeats = shards * heads_dev // HEADS
    stats = jnp.stack([maxima, totals_high, totals_low], 0)
    stats = jnp.repeat(stats, repeats, axis=2).reshape(3, all_rows, shards, heads_dev)
    stats = stats.transpose(2, 0, 3, 1).reshape(shards, 3 * heads_dev, all_rows)
    pieces = (
        numerators.astype(jnp.bfloat16)
        .reshape(all_rows, shards, columns_dev)
        .transpose(1, 0, 2)
    )
    lanes = -(-all_rows // columns_dev)
    stats = jnp.pad(stats, ((0, 0), (0, 0), (0, lanes * columns_dev - all_rows)))
    stats = stats.reshape(shards, 3 * heads_dev * lanes, columns_dev)
    got = lax.all_to_all(
        jnp.concatenate([pieces, stats], 1), "ctx", split_axis=0, concat_axis=0, tiled=True
    )
    parts = got[:, :all_rows].astype(jnp.float32)
    stats = got[:, all_rows:].reshape(shards, 3, heads_dev, lanes * columns_dev)[..., :all_rows]
    stats = stats.astype(jnp.float32)
    maxima, totals = stats[:, 0], stats[:, 1] + stats[:, 2]
    largest = jnp.max(maxima, axis=0)
    rescale = jnp.exp(maxima - largest)
    scale = rescale / jnp.sum(totals * rescale, axis=0)
    scale = jnp.repeat(scale.transpose(0, 2, 1), columns_dev // heads_dev, axis=2)
    columns = jnp.sum(parts * scale, axis=0).astype(jnp.bfloat16)
    projected = jnp.dot(columns, out_weight, preferred_element_type=jnp.float32)
    received = lax.all_to_all(
        projected.astype(jnp.bfloat16).reshape(shards, rows_dev, width),
        "ctx",
        split_axis=0,
        concat_axis=0,
        tiled=True,
    )
    projected = jnp.sum(received.astype(jnp.float32), axis=0)
    state = residual_in.astype(jnp.float32) + projected
    normed = (
        state
        * lax.rsqrt(jnp.mean(state * state, axis=1, keepdims=True) + epsilon)
        * norm_gain.astype(jnp.float32)
    ).astype(jnp.bfloat16)
    every = spread(normed, shards).reshape(all_rows, width)
    gate_out = jnp.dot(every, expert_gate[0], preferred_element_type=jnp.float32)
    up_out = jnp.dot(every, expert_up[0], preferred_element_type=jnp.float32)
    activated = (jax.nn.silu(gate_out) * up_out).astype(jnp.bfloat16)
    expert_out = jnp.dot(
        activated, expert_down[0], preferred_element_type=jnp.float32
    ).astype(jnp.bfloat16)
    back = lax.all_to_all(
        expert_out.reshape(shards, rows_dev, width), "ctx", split_axis=0, concat_axis=0, tiled=True
    )
    experts = jnp.arange(shards, dtype=jnp.int32)
    chosen = jnp.sum(
        jnp.where(
            expert_ids[:, :, None] == experts[None, None, :], expert_weights[:, :, None], 0.0
        ),
        axis=1,
    )
    expert_sum = jnp.sum(back.astype(jnp.float32) * chosen.T[:, :, None], axis=0)
    return (state + expert_sum).astype(jnp.bfloat16)


def solution(mesh):
    placed = (
        P(("groups", "ctx"), None),
        P(("groups", "ctx"), None),
        P(("groups", "ctx"), None),
        P(("groups", "ctx"), None),
        P(("groups", "ctx"), None),
        P(("groups", "ctx")),
        P(("groups", "ctx"), None),
        P("ctx", None),
        P(),
        P("ctx", None, None),
        P("ctx", None, None),
        P("ctx", None, None),
        P(("groups", "ctx"), None),
        P(("groups", "ctx"), None),
    )
    return jax.shard_map(
        local, mesh=mesh, in_specs=placed, out_specs=P(("groups", "ctx"), None), check_vma=False
    )
```

time: 360 us -> 110 us (0.31)
  blocking collectives: 168 us -> 30.5 us
  waiting for transfers between devices: 143 us -> 31.5 us
  starting transfers between devices: 0.04 us -> 14.8 us
  between operations: 15 us -> 0.9 us
  local copies, waits for them, and re-layouts: 7.41 us -> 14.8 us
  matrix products: 14.8 us -> 9.84 us
  other arithmetic: 10.8 us -> 6.78 us
    unnamed x3 -> x0, waiting for transfers between devices: 89.5 us -> none
    pmax x1 -> x0, blocking collectives: 57.8 us -> none  [local(): largest = lax.pmax(maxima, 'ctx')]
    psum x1 -> x0, blocking collectives: 57.6 us -> none  [local(): denoms = lax.psum(totals * rescale, 'ctx')]
    reduce_scatter x1 -> x0, waiting for transfers between devices: 53.7 us -> none  [local(): lax.psum_scatter(weighted, 'ctx', scatter_dimension=1, tiled=True)]
    all_to_all x0 -> x3, waiting for transfers between devices: none -> 31.5 us  [the longest x1 12.5 us: spread(): lax.all_to_all(copies, 'ctx', split_axis=0, concat_axis=0, tiled=True)]
    all_gather x1 -> x0, blocking collectives: 26.4 us -> none  [local(): whole_queries = lax.all_gather(queries, 'ctx', axis=0, tiled=True)]
    all_to_all x0 -> x3, starting transfers between devices: none -> 14.8 us  [the longest x1 7.47 us: spread(): lax.all_to_all(copies, 'ctx', split_axis=0, concat_axis=0, tiled=True)]
    all_to_all x2, blocking collectives: 26.5 us -> 30.5 us  [the longest x1 17.2 us: local(): lax.all_to_all(jnp.concatenate([pieces, stats], 1), 'ctx', split_axis=0,...]
  transfers between devices with their start and end apart: 2 -> 3, of which waited for: 2 -> 3; matrix products, arithmetic and copies ran while one was open for 0% -> 2% of each run, Pallas kernels for 0% -> 0%
where the time goes in v1:
time: 110 us; the launch traced here: 109 us
  waiting for transfers between devices  31.5 us (29%)
  blocking collectives  30.5 us (28%)
  local copies, waits for them, and re-layouts  14.8 us (13%)
  starting transfers between devices  14.8 us (13%)
  matrix products  9.84 us (9%)
  other arithmetic  6.78 us (6%)
    all_to_all x1, blocking collectives, local(): lax.all_to_all(jnp.concatenate([pieces, stats], 1), 'ctx', split_axis=0,...  17.2 us
    all_to_all x1, blocking collectives, spread(): lax.all_to_all(copies, 'ctx', split_axis=0, concat_axis=0, tiled=True)  13.3 us
    all_to_all x1, waiting for transfers between devices, spread(): lax.all_to_all(copies, 'ctx', split_axis=0, concat_axis=0, tiled=True)  12.5 us
    all_to_all x1, waiting for transfers between devices, local(): lax.all_to_all(projected.astype(jnp.bfloat16).reshape(shards, rows_dev, w...  9.99 us
    all_to_all x1, waiting for transfers between devices, local(): lax.all_to_all(expert_out.reshape(shards, rows_dev, width), 'ctx', split_...  9.11 us
    all_to_all x1, starting transfers between devices, spread(): lax.all_to_all(copies, 'ctx', split_axis=0, concat_axis=0, tiled=True)  7.47 us
    all_to_all x1, starting transfers between devices, local(): lax.all_to_all(projected.astype(jnp.bfloat16).reshape(shards, rows_dev, w...  3.8 us
    all_to_all x1, starting transfers between devices, local(): lax.all_to_all(expert_out.reshape(shards, rows_dev, width), 'ctx', split_...  3.53 us
  transfers between devices with their start and end apart: 3, of which 3 were waited for; matrix products, arithmetic and copies ran while one was open for 2% of the time, Pallas kernels for 0%

profile of v1, /device:TPU:0, one launch (start us, length us, event | category | flops | bytes accessed | tf_op | source)
XLA Modules:
  0.0 109.1 jit_solution(9250552965431761330)
XLA Ops:
  0.0 1.9 %broadcast_in_dim.71 = bf16[16,3,4096]{2,1,0:T(4,128)(2,1)} broadcast(bf16[3,4096]{1,0:T(4,128)(2,1)} %param.14), dimensions={1,2} | broadcast | bytes 417792 | tf_op jit(solution)/shard_map/broadcast_in_dim | solution.py:17
  1.9 7.5 %all-to-all-start = ((bf16[16,3,4096]{2,1,0:T(4,128)(2,1)}), bf16[16,3,4096]{2,1,0:T(4,128)(2,1)}, u32[]{:S(2)}, u32[]{:S(2)}) async-start(bf16[16,3,4096]{2,1,0:T(4,128)(2,1)} %broadcast_in_dim.71), calls=%async_computation | async-start | bytes 1048576 | tf_op jit(solution)/shard_map/all_to_all | solution.py:18
  10.2 0.9 pad_maximum_fusion
  11.3 12.5 %all-to-all-done = bf16[16,3,4096]{2,1,0:T(4,128)(2,1)} async-done(((bf16[16,3,4096]{2,1,0:T(4,128)(2,1)}), bf16[16,3,4096]{2,1,0:T(4,128)(2,1)}, u32[]{:S(2)}, u32[]{:S(2)}) %all-to-all-start) | async-done | bytes 393248 | tf_op jit(solution)/shard_map/all_to_all | solution.py:18
  23.7 2.2 %reshape_reshape.3 = bf16[48,4,8,128]{3,2,1,0:T(8,128)(2,1)} reshape(bf16[16,3,4096]{2,1,0:T(4,128)(2,1)} %all-to-all-done) | data formatting | bytes 786432 | tf_op jit(solution)/shard_map/reshape;reshape | solution.py:44
  25.9 1.5 %fusion.47 = (bf16[4,8,48]{2,1,0:T(8,128)(2,1)S(1)}, f32[4,8,48,131]{3,2,1,0:T(8,128)S(1)}) fusion(bf16[48,4,8,128]{3,2,1,0:T(8,128)(2,1)} %reshape_reshape.3, bf16[131,4,128,1]{2,1,0,3:T(4,128)(2,1)S(1)} %bitcast.65, pred[48,131]{1,0:T(8,128)(4,1)S(1)} %fusion.38), kind=kOutput, calls=%fused_computation.64 | convolution fusion | flops 52113408 | bytes 1341584 | tf_op jit(solution)/shard_map/rkgd,nkd->kgrn/dot_general | solution.py:60
  27.5 0.5 fusion.10
  28.1 0.6 copy.47
  28.7 0.4 fusion.12
  29.3 0.9 convert_element_type.113
  30.1 1.0 fusion.28
  31.3 17.2 %all_to_all.25 = bf16[16,54,256]{2,1,0:T(8,128)(2,1)S(1)} all-to-all(bf16[16,54,256]{2,1,0:T(8,128)(2,1)S(1)} %copy.48), channel_id=1, replica_groups=mesh['groups'=2,'ctx'=16] {'ctx'}, dimensions={0} | all-to-all | bytes 884736 | tf_op jit(solution)/shard_map/all_to_all | solution.py:92
  48.5 0.8 copy-done.1
  49.4 0.2 copy.50
  49.6 1.7 %broadcast_in_dim.74 = f32[16,48,2,128]{3,2,1,0:T(2,128)} broadcast(f32[16,48,2]{2,1,0:T(8,128)S(1)} %copy.50), dimensions={0,1,2} | broadcast | bytes 792576 | tf_op jit(solution)/shard_map/broadcast_in_dim | solution.py:102
  51.4 2.6 %reshape.106 = f32[16,48,256]{2,1,0:T(8,128)} reshape(f32[16,48,2,128]{3,2,1,0:T(2,128)} %broadcast_in_dim.74) | data formatting | bytes 1572864 | tf_op jit(solution)/shard_map/reshape | solution.py:102
  54.0 1.3 %multiply_reduce_fusion = bf16[48,256]{1,0:T(8,128)(2,1)S(1)} fusion(f32[16,48,256]{2,1,0:T(8,128)} %reshape.106, bf16[16,54,256]{2,1,0:T(8,128)(2,1)} %copy-done.1), kind=kLoop, calls=%fused_computation.21 | loop fusion | flops 577536 | bytes 1204224 | tf_op jit(solution)/shard_map/reduce_sum | solution.py:103
  55.4 1.5 %convolution_convert_fusion = bf16[48,2048]{1,0:T(8,128)(2,1)S(1)} fusion(bf16[256,2048]{1,0:T(8,128)(2,1)} %param.21, bf16[48,256]{1,0:T(8,128)(2,1)S(1)} %multiply_reduce_fusion), kind=kOutput, calls=%fused_computation.8 | convolution fusion | flops 50429952 | bytes 1269760 | tf_op jit(solution)/shard_map/dot_general | solution.py:104
  56.9 0.8 reshape.107
  57.7 3.8 %all-to-all-start.2 = ((bf16[16,3,2048]{2,1,0:T(4,128)(2,1)}), bf16[16,3,2048]{2,1,0:T(4,128)(2,1)S(1)}, u32[]{:S(2)}, u32[]{:S(2)}) async-start(bf16[16,3,2048]{2,1,0:T(4,128)(2,1)} %reshape.107), calls=%async_computation.2 | async-start | bytes 524288 | tf_op jit(solution)/shard_map/all_to_all | solution.py:105
  61.5 10.0 %all-to-all-done.2 = bf16[16,3,2048]{2,1,0:T(4,128)(2,1)S(1)} async-done(((bf16[16,3,2048]{2,1,0:T(4,128)(2,1)}), bf16[16,3,2048]{2,1,0:T(4,128)(2,1)S(1)}, u32[]{:S(2)}, u32[]{:S(2)}) %all-to-all-start.2) | async-done | bytes 196640 | tf_op jit(solution)/shard_map/all_to_all | solution.py:105
  71.8 0.4 copy-done.2
  72.4 13.3 %all_to_all.26 = bf16[16,3,2048]{2,1,0:T(4,128)(2,1)} all-to-all(bf16[16,3,2048]{2,1,0:T(4,128)(2,1)S(1)} %broadcast_in_dim.75), channel_id=1, replica_groups=mesh['groups'=2,'ctx'=16] {'ctx'}, dimensions={0} | all-to-all | bytes 393216 | tf_op jit(solution)/shard_map/all_to_all | solution.py:18
  85.7 1.1 %reshape.108 = bf16[48,2048]{1,0:T(8,128)(2,1)S(1)} reshape(bf16[16,3,2048]{2,1,0:T(4,128)(2,1)} %all_to_all.26) | data formatting | bytes 393216 | tf_op jit(solution)/shard_map/reshape | solution.py:119
  86.8 3.2 %fusion.5 = f32[48,768]{1,0:T(8,128)} fusion(bf16[48,2048]{1,0:T(8,128)(2,1)S(1)} %reshape.108, bf16[1,2048,768]{2,1,0:T(8,128)(2,1)} %param.23), kind=kOutput, calls=%fused_computation.5 | convolution fusion | flops 150994944 | bytes 3489792 | tf_op jit(solution)/shard_map/dot_general | solution.py:120
  90.0 3.2 %fusion.7 = bf16[48,2048]{1,0:T(8,128)(2,1)S(1)} fusion(bf16[1,768,2048]{2,1,0:T(8,128)(2,1)S(1)} %copy-done, bf16[48,2048]{1,0:T(8,128)(2,1)S(1)} %reshape.108, bf16[1,2048,768]{2,1,0:T(8,128)(2,1)} %param.24, f32[48,768]{1,0:T(8,128)} %fusion.5), kind=kOutput, calls=%fused_computation.7 | convolution fusion | flops 302309376 | bytes 6832128 | tf_op jit(solution)/shard_map/dot_general | solution.py:123
  93.2 0.8 reshape.109
  94.0 3.5 %all-to-all-start.4 = ((bf16[16,3,2048]{2,1,0:T(4,128)(2,1)}), bf16[16,3,2048]{2,1,0:T(4,128)(2,1)S(1)}, u32[]{:S(2)}, u32[]{:S(2)}) async-start(bf16[16,3,2048]{2,1,0:T(4,128)(2,1)} %reshape.109), calls=%async_computation.4 | async-start | bytes 524288 | tf_op jit(solution)/shard_map/all_to_all | solution.py:126
  97.6 0.8 select_reduce_fusion
  98.5 9.1 %all-to-all-done.4 = bf16[16,3,2048]{2,1,0:T(4,128)(2,1)S(1)} async-done(((bf16[16,3,2048]{2,1,0:T(4,128)(2,1)}), bf16[16,3,2048]{2,1,0:T(4,128)(2,1)S(1)}, u32[]{:S(2)}, u32[]{:S(2)}) %all-to-all-start.4) | async-done | bytes 196640 | tf_op jit(solution)/shard_map/all_to_all | solution.py:126
  107.6 0.2 multiply_reduce_fusion.1
  107.8 1.4 %add_convert_fusion = bf16[3,2048]{1,0:T(4,128)(2,1)} fusion(f32[3,2048]{1,0:T(4,128)S(1)} %multiply_reduce_fusion.1, f32[3,2048]{1,0:T(4,128)} %copy-done.2, bf16[3,2048]{1,0:T(4,128)(2,1)S(1)} %copy-done.3), kind=kLoop, calls=%fused_computation.41 | loop fusion | flops 24576 | bytes 73728 | tf_op jit(solution)/shard_map/convert_element_type | solution.py:137
  (35 shorter events, 1.2 us)
Async XLA Ops:
  0.0 90.0 %copy-start = (bf16[1,768,2048]{2,1,0:T(8,128)(2,1)S(1)}, bf16[1,768,2048]{2,1,0:T(8,128)(2,1)}, u32[]{:S(2)}) copy-start(bf16[1,768,2048]{2,1,0:T(8,128)(2,1)} %param.25) | copy-start | bytes 9437188
  0.0 10.1 %copy-start.4 = (bf16[128,512]{1,0:T(8,128)(2,1)S(1)}, bf16[128,512]{1,0:T(8,128)(2,1)}, u32[]{:S(2)}) copy-start(bf16[128,512]{1,0:T(8,128)(2,1)} %param.15) | copy-start | bytes 393220
  0.0 10.1 %copy-start.5 = (bf16[3,512]{1,0:T(4,128)(2,1)S(1)}, bf16[3,512]{1,0:T(4,128)(2,1)}, u32[]{:S(2)}) copy-start(bf16[3,512]{1,0:T(4,128)(2,1)} %param.17) | copy-start | bytes 9220
  1.9 21.8 %all-to-all-start = ((bf16[16,3,4096]{2,1,0:T(4,128)(2,1)}), bf16[16,3,4096]{2,1,0:T(4,128)(2,1)}, u32[]{:S(2)}, u32[]{:S(2)}) async-start(bf16[16,3,4096]{2,1,0:T(4,128)(2,1)} %broadcast_in_dim.71), calls=%async_computation | async-start | bytes 1048576 | tf_op jit(solution)/shard_map/all_to_all | solution.py:18
  48.5 0.8 copy-start.1
  54.0 7.5 %copy-start.6 = (bf16[2048]{0:T(1024)(128)(2,1)S(1)}, bf16[2048]{0:T(1024)(128)(2,1)}, u32[]{:S(2)}) copy-start(bf16[2048]{0:T(1024)(128)(2,1)} %param.22) | copy-start | bytes 12292
  55.3 16.3 %copy-start.3 = (bf16[3,2048]{1,0:T(4,128)(2,1)S(1)}, bf16[3,2048]{1,0:T(4,128)(2,1)}, u32[]{:S(2)}) copy-start(bf16[3,2048]{1,0:T(4,128)(2,1)} %param.20) | copy-start | bytes 36868
  57.7 13.8 %all-to-all-start.2 = ((bf16[16,3,2048]{2,1,0:T(4,128)(2,1)}), bf16[16,3,2048]{2,1,0:T(4,128)(2,1)S(1)}, u32[]{:S(2)}, u32[]{:S(2)}) async-start(bf16[16,3,2048]{2,1,0:T(4,128)(2,1)} %reshape.107), calls=%async_computation.2 | async-start | bytes 524288 | tf_op jit(solution)/shard_map/all_to_all | solution.py:105
  71.7 0.6 copy-start.2
  94.0 13.5 %all-to-all-start.4 = ((bf16[16,3,2048]{2,1,0:T(4,128)(2,1)}), bf16[16,3,2048]{2,1,0:T(4,128)(2,1)S(1)}, u32[]{:S(2)}, u32[]{:S(2)}) async-start(bf16[16,3,2048]{2,1,0:T(4,128)(2,1)} %reshape.109), calls=%async_computation.4 | async-start | bytes 524288 | tf_op jit(solution)/shard_map/all_to_all | solution.py:126
